TPU v7x, 256 devices: a whole 4x4x8 slice. The times are simulated.
256 devices in a mesh: seq: 32 (over y, z_lo, x), exp: 8 (over z_hi, core).
Axes of the slice: x: 4, y: 4, z: 8 (z_hi: 4, z_lo: 2; z = z_hi * 2 + z_lo), core: 2. Of those that a mesh axis runs over, the one named last changes fastest.
Arguments:
- query_input: bfloat16 [4096, 2048], P('seq', 'exp'), may hold values from -4.5 to 4.5
- key_input: bfloat16 [4096, 2048], P('seq', 'exp'), may hold values from -4.5 to 4.5
- value_input: bfloat16 [4096, 2048], P('seq', 'exp'), may hold values from -6 to 6
- segment_ids: int32 [4096], P('seq'), may hold values from 0 to 15, never falling along the last dimension, each value on 1 to 512 neighbouring positions
- residual_in: bfloat16 [4096, 4096], P('seq', 'exp'), may hold values from -13.5 to 13.5
- out_weight: bfloat16 [2048, 4096], P('exp'), may hold values from -0.1875 to 0.1875
- norm_gain: float32 [4096], P('exp'), may hold values from 0.1 to 1.9
- router: bfloat16 [4096, 32], P(None, 'seq'), may hold values from -0.1875 to 0.1875
- modality: int32 [4096], P('seq'), may hold values from 0 to 1
- expert_in: int32 [4096], P('seq'), may hold values from 0 to 15, as said below
- gate_weight: bfloat16 [32, 4096, 2816], P('seq', None, 'exp'), may hold values from -0.09375 to 0.09375
- up_weight: bfloat16 [32, 4096, 2816], P('seq', None, 'exp'), may hold values from -0.09375 to 0.09375
- down_weight: bfloat16 [32, 2816, 4096], P('seq', 'exp'), may hold values from -0.15625 to 0.15625
Outputs:
- layer_out: bfloat16 [4096, 4096], P('seq', 'exp')
Inputs may be any that keep to these rules, and one draw needn't show every extreme that they name: `segment_ids`: document numbers never fall along the sequence, and a document holds at most an eighth of the 4096 tokens. `expert_in`: within each aligned block of 128 tokens no expert (modality and number together) is chosen by more than 7 tokens, and in every block some expert is chosen by exactly 7.
All inputs are finite; a program needn't handle non-finite values.
Results may differ from a plain program's by a relative error of at most 0.0095.
Values may be sent and summed in bfloat16 or wider, within the bound.
A program may use at most 64 MiB of HBM per device.

v0:
```python
import jax
import jax.numpy as jnp
from jax import lax
from jax.sharding import Mesh
from jax.sharding import PartitionSpec as P

D = 4096
HEAD_DIM = 128
EXPERTS = 32
MODAL_EXPERTS = 16
CAPACITY = 7
EXP = ("exp_0", "exp_1")
NEGATIVE = -1e30
EPSILON = 1e-05


def passed_along(value, axis, steps):
    count = lax.axis_size(axis)
    leading, last = (max(0, -steps), min(count, count - steps))
    return lax.ppermute(value, axis, [(source, source + steps) for source in range(leading, last)])


def split_up(array, dim, length):
    lengths = array.shape
    tiles = array.reshape(*lengths[:dim], length, lengths[dim] // length, *lengths[dim + 1 :])
    return jnp.moveaxis(tiles, dim, 0)


def sent_and_summed(array, axis, dim):
    length = lax.axis_size(axis)
    tiles = lax.all_to_all(split_up(array, dim, length), axis, 0, 0, tiled=True)
    return jnp.sum(tiles.astype(jnp.float32), axis=0)


def copy_for_each(array, axis):
    copies = jnp.broadcast_to(array, (lax.axis_size(axis), *array.shape))
    return lax.all_to_all(copies, axis, split_axis=0, concat_axis=0, tiled=True)


def over_copies(array, axis):
    everything = copy_for_each(array, axis)
    return jnp.sum(everything, axis=0)


def joined_along(tiles, dim):
    tiles = jnp.moveaxis(tiles, 0, dim)
    lengths = tiles.shape
    return tiles.reshape(*lengths[:dim], lengths[dim] * lengths[dim + 1], *lengths[dim + 2 :])


def stacked_from(array, axes, turns):
    tiles = array
    for k in turns:
        tiles = lax.all_gather(tiles, axes[k])
    done = turns[::-1]
    back = [done.index(k) for k in range(len(axes))]
    tiles = tiles.transpose(*back, *range(len(axes), tiles.ndim))
    return tiles.reshape(-1, *array.shape)


def gather_axes(array, axes, turns, dim):
    return joined_along(stacked_from(array, axes, turns), dim)


def absorb(carry_state, query_heads, key_block, value_block, allowed):
    running_max, denominators, numerators = carry_state
    scores = jnp.einsum(
        "qhd,khd->hqk", query_heads, key_block, preferred_element_type=jnp.float32
    ) * HEAD_DIM ** (-0.5)
    masked = jnp.where(allowed[None], scores, NEGATIVE)
    new_max = jnp.maximum(running_max, jnp.max(masked, axis=2))
    rescale = jnp.exp(running_max - new_max)
    weights = jnp.exp(masked - new_max[:, :, None])
    denominators = denominators * rescale + jnp.sum(weights, axis=2)
    numerators = numerators * rescale[:, :, None] + jnp.einsum(
        "hqk,khd->hqd",
        weights.astype(jnp.bfloat16),
        value_block,
        preferred_element_type=jnp.float32,
    )
    return (new_max, denominators, numerators)


def local(
    query_input,
    key_input,
    value_input,
    segment_ids,
    residual_in,
    out_weight,
    norm_gain,
    router,
    modality,
    expert_in,
    gate_weight,
    up_weight,
    down_weight,
):
    token_count = query_input.shape[0]
    head_count = query_input.shape[1] // HEAD_DIM
    query_heads = query_input.reshape(token_count, head_count, HEAD_DIM)
    key_heads = key_input.reshape(token_count, head_count, HEAD_DIM)
    value_heads = value_input.reshape(token_count, head_count, HEAD_DIM)
    positions = jnp.arange(token_count, dtype=jnp.int32)
    local_mask = (segment_ids[:, None] == segment_ids[None, :]) & (
        positions[None, :] <= positions[:, None]
    )
    empty_state = (
        jnp.full((head_count, token_count), NEGATIVE, jnp.float32),
        jnp.zeros((head_count, token_count), jnp.float32),
        jnp.zeros((head_count, token_count, HEAD_DIM), jnp.float32),
    )
    carry_state = absorb(empty_state, query_heads, key_heads, value_heads, local_mask)
    cycle_index = lax.axis_index("seq")

    def visit(step_number, loop_carry):
        visit_state, key_block, value_block, travel_segments = loop_carry
        key_block, value_block, travel_segments = passed_along(
            (key_block, value_block, travel_segments), "seq", 1
        )
        has_block = cycle_index - step_number - 1 >= 0
        allowed = has_block & (segment_ids[:, None] == travel_segments.astype(jnp.int32)[None, :])
        visit_state = absorb(visit_state, query_heads, key_block, value_block, allowed)
        return (visit_state, key_block, value_block, travel_segments)

    start_carry = (carry_state, key_heads, value_heads, segment_ids.astype(jnp.bfloat16))
    final_carry = lax.fori_loop(0, lax.axis_size("seq") // 8, visit, start_carry)
    running_max, denominators, numerators = final_carry[0]
    attended = (numerators / denominators[:, :, None]).astype(jnp.bfloat16)
    attended = jnp.transpose(attended, (1, 0, 2)).reshape(token_count, head_count * HEAD_DIM)
    projected = jnp.dot(attended, out_weight, preferred_element_type=jnp.float32)
    attention = sent_and_summed(projected.astype(jnp.bfloat16), EXP, 1)
    residual = residual_in.astype(jnp.float32) + attention
    squares = jnp.sum(residual * residual, axis=1)
    square_total = over_copies(squares, EXP)
    normed = (residual * lax.rsqrt(square_total / D + EPSILON)[:, None] * norm_gain).astype(
        jnp.bfloat16
    )
    picked = modality * MODAL_EXPERTS + expert_in
    one_hot = (picked[:, None] == jnp.arange(EXPERTS, dtype=jnp.int32)[None, :]).astype(jnp.int32)
    rank_in_block = jnp.sum(one_hot * (jnp.cumsum(one_hot, axis=0) - 1), axis=1)
    slot_index = picked * CAPACITY + rank_in_block
    outgoing = (
        jnp.zeros((EXPERTS * CAPACITY, normed.shape[1]), jnp.bfloat16).at[slot_index].set(normed)
    )
    sliced = lax.all_to_all(
        outgoing.reshape(EXPERTS, CAPACITY, normed.shape[1]),
        "seq",
        split_axis=0,
        concat_axis=1,
        tiled=True,
    )
    arrived = gather_axes(sliced, EXP, (0, 1), 2)
    gate_sum = jnp.einsum("erd,edf->erf", arrived, gate_weight, preferred_element_type=jnp.float32)
    up_sum = jnp.einsum("erd,edf->erf", arrived, up_weight, preferred_element_type=jnp.float32)
    logits = jnp.einsum("erd,de->er", arrived, router, preferred_element_type=jnp.float32)
    hidden = (jax.nn.silu(gate_sum) * up_sum * jax.nn.sigmoid(logits)[:, :, None]).astype(
        jnp.bfloat16
    )
    partial_value = jnp.einsum(
        "erf,efd->erd", hidden, down_weight, preferred_element_type=jnp.float32
    )
    summed = lax.psum_scatter(
        partial_value.astype(jnp.bfloat16), EXP, scatter_dimension=2, tiled=True
    )
    returned = lax.all_to_all(summed, "seq", split_axis=1, concat_axis=0, tiled=True)
    routed = returned.reshape(EXPERTS * CAPACITY, returned.shape[2])[slot_index]
    return (residual + routed.astype(jnp.float32)).astype(jnp.bfloat16)


def solution(mesh):
    split = Mesh(mesh.devices.reshape(mesh.shape["seq"], 4, 2), ("seq", "exp_0", "exp_1"))
    placed = (
        P("seq", EXP),
        P("seq", EXP),
        P("seq", EXP),
        P("seq"),
        P("seq", EXP),
        P(EXP, None),
        P(EXP),
        P(None, "seq"),
        P("seq"),
        P("seq"),
        P("seq", None, EXP),
        P("seq", None, EXP),
        P("seq", EXP, None),
    )
    return jax.shard_map(
        local, mesh=split, in_specs=placed, out_specs=P("seq", EXP), check_vma=False
    )
```

profile of v0, /device:TPU:2, one launch (start us, length us, event | category | flops | bytes accessed | tf_op | source)
XLA Modules:
  0.0 265.8 jit_solution(9415738646136405745)
XLA Ops:
  6.5 0.9 fusion.41
  7.4 0.7 convert_element_type.62
  8.1 0.9 copy.78
  9.1 1.0 copy.79
  10.3 0.2 fusion.44
  10.6 1.0 copy.82
  11.7 0.2 convolution_add_fusion.1
  11.9 56.5 %while.25 = (s32[]{:T(128)}, f32[2,128]{1,0:T(2,128)S(1)}, f32[2,128]{1,0:T(2,128)S(1)}, f32[2,128,128]{2,1,0:T(8,128)S(1)}, bf16[128,2,128]{2,0,1:T(8,128)(2,1)...) while((s32[]{:T(128)}, f32[2,128]{1,0:T(2,128)S(1)}, ...), condition=%wide.region_5.6_spmd, body=%wide.region_2.5_spmd.sunk | while | flops 17171076 | bytes 1723927 | solution.py:127
  11.9 3.4 %collective-permute-start = (bf16[128]{0:T(256)(128)(2,1)S(1)}, bf16[128]{0:T(256)(128)(2,1)S(1)}, u32[]{:S(2)}, u32[]{:S(2)}) collective-permute-start(bf16[128]{0:T(256)(128)(2,1)S(1)} %get-tuple-element.416), channel_id=1, source_target_pairs={{0,8},{8,16},{16,24},{24,32},{32,40},{40,48},{48,56},{56,64},{64,7... | collective-permute-start | bytes 776 | tf_op jit(solution)/shard_map/while/body/eval_jaxpr/ppermute | solution.py:20
  15.3 3.1 %collective-permute-start.1 = (bf16[128,2,128]{2,0,1:T(8,128)(2,1)S(1)}, bf16[128,2,128]{2,0,1:T(8,128)(2,1)S(1)}, u32[]{:S(2)}, u32[]{:S(2)}) collective-permute-start(bf16[128,2,128]{2,0,1:T(8,128)(2,1)S(1)} %get-tuple-element.414), channel_id=1, source_target_pairs={{0,8},{8,16},{16,24},{24,32},{32,40},{40,48},{48,56},{56,64},{64,7... | collective-permute-start | bytes 196616 | tf_op jit(solution)/shard_map/while/body/eval_jaxpr/ppermute | solution.py:20
  18.5 3.7 %collective-permute-start.2 = (bf16[128,2,128]{2,0,1:T(8,128)(2,1)S(1)}, bf16[128,2,128]{2,0,1:T(8,128)(2,1)S(1)}, u32[]{:S(2)}, u32[]{:S(2)}) collective-permute-start(bf16[128,2,128]{2,0,1:T(8,128)(2,1)S(1)} %get-tuple-element.415), channel_id=1, source_target_pairs={{0,8},{8,16},{16,24},{24,32},{32,40},{40,48},{48,56},{56,64},{64,7... | collective-permute-start | bytes 196616 | tf_op jit(solution)/shard_map/while/body/eval_jaxpr/ppermute | solution.py:20
  22.2 0.7 compare_and_fusion.2
  23.0 0.2 select_reduce_fusion.3
  23.3 1.3 collective-permute-done.2
  24.6 0.2 convolution_add_fusion.3
  24.9 3.7 %collective-permute-start = (bf16[128]{0:T(256)(128)(2,1)S(1)}, bf16[128]{0:T(256)(128)(2,1)S(1)}, u32[]{:S(2)}, u32[]{:S(2)}) collective-permute-start(bf16[128]{0:T(256)(128)(2,1)S(1)} %get-tuple-element.416), channel_id=1, source_target_pairs={{0,8},{8,16},{16,24},{24,32},{32,40},{40,48},{48,56},{56,64},{64,7... | collective-permute-start | bytes 776 | tf_op jit(solution)/shard_map/while/body/eval_jaxpr/ppermute | solution.py:20
  28.6 3.4 %collective-permute-start.1 = (bf16[128,2,128]{2,0,1:T(8,128)(2,1)S(1)}, bf16[128,2,128]{2,0,1:T(8,128)(2,1)S(1)}, u32[]{:S(2)}, u32[]{:S(2)}) collective-permute-start(bf16[128,2,128]{2,0,1:T(8,128)(2,1)S(1)} %get-tuple-element.414), channel_id=1, source_target_pairs={{0,8},{8,16},{16,24},{24,32},{32,40},{40,48},{48,56},{56,64},{64,7... | collective-permute-start | bytes 196616 | tf_op jit(solution)/shard_map/while/body/eval_jaxpr/ppermute | solution.py:20
  32.0 5.5 %collective-permute-start.2 = (bf16[128,2,128]{2,0,1:T(8,128)(2,1)S(1)}, bf16[128,2,128]{2,0,1:T(8,128)(2,1)S(1)}, u32[]{:S(2)}, u32[]{:S(2)}) collective-permute-start(bf16[128,2,128]{2,0,1:T(8,128)(2,1)S(1)} %get-tuple-element.415), channel_id=1, source_target_pairs={{0,8},{8,16},{16,24},{24,32},{32,40},{40,48},{48,56},{56,64},{64,7... | collective-permute-start | bytes 196616 | tf_op jit(solution)/shard_map/while/body/eval_jaxpr/ppermute | solution.py:20
  37.6 0.7 compare_and_fusion.2
  38.7 0.8 collective-permute-done.2
  39.5 0.2 convolution_add_fusion.3
  39.7 4.3 %collective-permute-start = (bf16[128]{0:T(256)(128)(2,1)S(1)}, bf16[128]{0:T(256)(128)(2,1)S(1)}, u32[]{:S(2)}, u32[]{:S(2)}) collective-permute-start(bf16[128]{0:T(256)(128)(2,1)S(1)} %get-tuple-element.416), channel_id=1, source_target_pairs={{0,8},{8,16},{16,24},{24,32},{32,40},{40,48},{48,56},{56,64},{64,7... | collective-permute-start | bytes 776 | tf_op jit(solution)/shard_map/while/body/eval_jaxpr/ppermute | solution.py:20
  44.0 1.9 collective-permute-start.1
  45.9 4.1 %collective-permute-start.2 = (bf16[128,2,128]{2,0,1:T(8,128)(2,1)S(1)}, bf16[128,2,128]{2,0,1:T(8,128)(2,1)S(1)}, u32[]{:S(2)}, u32[]{:S(2)}) collective-permute-start(bf16[128,2,128]{2,0,1:T(8,128)(2,1)S(1)} %get-tuple-element.415), channel_id=1, source_target_pairs={{0,8},{8,16},{16,24},{24,32},{32,40},{40,48},{48,56},{56,64},{64,7... | collective-permute-start | bytes 196616 | tf_op jit(solution)/shard_map/while/body/eval_jaxpr/ppermute | solution.py:20
  50.1 0.7 compare_and_fusion.2
  51.2 0.9 collective-permute-done.2
  52.1 0.2 convolution_add_fusion.3
  52.4 4.1 %collective-permute-start = (bf16[128]{0:T(256)(128)(2,1)S(1)}, bf16[128]{0:T(256)(128)(2,1)S(1)}, u32[]{:S(2)}, u32[]{:S(2)}) collective-permute-start(bf16[128]{0:T(256)(128)(2,1)S(1)} %get-tuple-element.416), channel_id=1, source_target_pairs={{0,8},{8,16},{16,24},{24,32},{32,40},{40,48},{48,56},{56,64},{64,7... | collective-permute-start | bytes 776 | tf_op jit(solution)/shard_map/while/body/eval_jaxpr/ppermute | solution.py:20
  56.5 3.4 %collective-permute-start.1 = (bf16[128,2,128]{2,0,1:T(8,128)(2,1)S(1)}, bf16[128,2,128]{2,0,1:T(8,128)(2,1)S(1)}, u32[]{:S(2)}, u32[]{:S(2)}) collective-permute-start(bf16[128,2,128]{2,0,1:T(8,128)(2,1)S(1)} %get-tuple-element.414), channel_id=1, source_target_pairs={{0,8},{8,16},{16,24},{24,32},{32,40},{40,48},{48,56},{56,64},{64,7... | collective-permute-start | bytes 196616 | tf_op jit(solution)/shard_map/while/body/eval_jaxpr/ppermute | solution.py:20
  59.9 6.4 %collective-permute-start.2 = (bf16[128,2,128]{2,0,1:T(8,128)(2,1)S(1)}, bf16[128,2,128]{2,0,1:T(8,128)(2,1)S(1)}, u32[]{:S(2)}, u32[]{:S(2)}) collective-permute-start(bf16[128,2,128]{2,0,1:T(8,128)(2,1)S(1)} %get-tuple-element.415), channel_id=1, source_target_pairs={{0,8},{8,16},{16,24},{24,32},{32,40},{40,48},{48,56},{56,64},{64,7... | collective-permute-start | bytes 196616 | tf_op jit(solution)/shard_map/while/body/eval_jaxpr/ppermute | solution.py:20
  66.3 0.7 compare_and_fusion.2
  67.4 0.8 collective-permute-done.2
  68.2 0.2 convolution_add_fusion.3
  68.6 2.1 convolution_convert_fusion.1
  70.7 1.1 copy.106
  71.8 8.6 %all-to-all-start = ((bf16[8,128,512]{2,1,0:T(8,128)(2,1)}), bf16[8,128,512]{2,1,0:T(8,128)(2,1)}, u32[]{:S(2)}, u32[]{:S(2)}) async-start(bf16[8,128,512]{2,1,0:T(8,128)(2,1)} %bitcast.76), calls=%async_computation | async-start | bytes 2097152 | tf_op jit(solution)/shard_map/all_to_all | solution.py:31
  80.9 28.9 %all-to-all-done = bf16[8,128,512]{2,1,0:T(8,128)(2,1)} async-done(((bf16[8,128,512]{2,1,0:T(8,128)(2,1)}), bf16[8,128,512]{2,1,0:T(8,128)(2,1)}, u32[]{:S(2)}, u32[]{:S(2)}) %all-to-all-start) | async-done | bytes 1048608 | tf_op jit(solution)/shard_map/all_to_all | solution.py:31
  109.8 1.4 convert_reduce_fusion
  111.3 0.6 broadcast_in_dim.92
  111.9 3.3 %all-to-all-start.1 = ((f32[8,1,128]{2,1,0:T(1,128)}), f32[8,1,128]{2,1,0:T(1,128)S(1)}, u32[]{:S(2)}, u32[]{:S(2)}) async-start(f32[8,1,128]{2,1,0:T(1,128)} %broadcast_in_dim.92), calls=%async_computation.1 | async-start | bytes 8192 | tf_op jit(solution)/shard_map/all_to_all | solution.py:37
  115.3 7.5 %all-to-all-done.1 = f32[8,1,128]{2,1,0:T(1,128)S(1)} async-done(((f32[8,1,128]{2,1,0:T(1,128)}), f32[8,1,128]{2,1,0:T(1,128)S(1)}, u32[]{:S(2)}, u32[]{:S(2)}) %all-to-all-start.1) | async-done | bytes 4128 | tf_op jit(solution)/shard_map/all_to_all | solution.py:37
  122.8 1.2 scatter_custom_fusion
  124.0 0.8 reshape.170
  124.8 16.9 %all_to_all.29 = bf16[32,7,512]{2,1,0:T(8,128)(2,1)} all-to-all(bf16[32,7,512]{2,1,0:T(8,128)(2,1)} %reshape.170), channel_id=1, replica_groups=mesh['seq'=32,'exp_0'=4,'exp_1'=2] {'seq'}, dimensions={0} | all-to-all | bytes 458752 | tf_op jit(solution)/shard_map/all_to_all | solution.py:146
  141.6 1.0 all_gather.12
  142.7 20.1 %all_gather.13 = bf16[4,1,224,512]{3,2,1,0:T(8,128)(2,1)} all-gather(bf16[1,1,224,512]{3,2,1,0:T(8,128)(2,1)S(1)} %all_gather.12), channel_id=1, replica_groups=mesh['seq'=32,'exp_0'=4,'exp_1'=2] {'exp_0'}, dimensions={0}, use_global_device_ids=true | all-gather | bytes 1146880 | tf_op jit(solution)/shard_map/all_gather | solution.py:54
  162.8 12.2 %all-gather.3.cloned.1.call-done = bf16[8,1,224,512]{3,2,1,0:T(8,128)(2,1)} async-done(((bf16[4,1,224,512]{3,2,1,0:T(8,128)(2,1)}), bf16[8,1,224,512]{3,2,1,0:T(8,128)(2,1)}) %all-gather.3.cloned.1.call-update) | async-done | bytes 1835024 | tf_op jit(solution)/shard_map/all_gather | solution.py:54
  175.0 1.7 copy.91
  176.7 0.2 copy.101
  177.0 2.2 copy-done.5
  179.2 1.9 fusion.11
  181.1 0.6 fusion.45
  181.7 6.1 %fusion.7 = bf16[1,224,4096]{2,1,0:T(8,128)(2,1)} fusion(bf16[1,352,4096]{2,1,0:T(8,128)(2,1)S(1)} %copy-done, bf16[224,4096]{1,0:T(8,128)(2,1)} %bitcast.72, bf16[1,4096,352]{1,2,0:T(8,128)(2,1)} %param.26, f32[224,352]{1,0:T(8,128)} %fusion.11, f32[224]{0:T(256)S(1)} %add_divide_fusion), kind=kOutput, calls=%fused_computation.16 | convolution fusion | flops 1293315072 | bytes 9753472 | tf_op jit(solution)/shard_map/erf,efd->erd/dot_general | solution.py:160
  187.9 44.3 %reduce-scatter.2.cloned.1.call-done = bf16[1,224,512]{2,1,0:T(8,128)(2,1)} async-done(((bf16[1,224,4096]{2,1,0:T(8,128)(2,1)}), bf16[1,224,512]{2,1,0:T(8,128)(2,1)}) %reduce-scatter.2.cloned.1.call-update) | async-done | bytes 229392 | tf_op jit(solution)/shard_map/reduce_scatter | solution.py:163
  232.1 2.1 copy.108
  234.2 0.5 broadcast.146
  234.7 2.9 %reduce.1 = bf16[224,512]{1,0:T(8,128)(2,1)S(1)} reduce(bf16[224,1,512]{2,1,0:T(2,128)(2,1)} %bitcast.78, bf16[]{:T(256)} %broadcast.146), dimensions={1}, to_apply=%bitcast.63.reduce_sub_computation | reduce | bytes 458754
  237.6 0.8 reshape.202
  238.4 7.4 %all-to-all-start.3 = ((bf16[32,2,1792]{2,1,0:T(2,128)(2,1)}), bf16[32,2,1792]{2,1,0:T(2,128)(2,1)S(1)}, u32[]{:S(2)}, u32[]{:S(2)}) async-start(bf16[32,2,1792]{2,1,0:T(2,128)(2,1)} %reshape.202), calls=%async_computation.4 | async-start | bytes 458752 | tf_op jit(solution)/shard_map/all_to_all | solution.py:166
  245.9 8.0 %all-to-all-done.3 = bf16[32,2,1792]{2,1,0:T(2,128)(2,1)S(1)} async-done(((bf16[32,2,1792]{2,1,0:T(2,128)(2,1)}), bf16[32,2,1792]{2,1,0:T(2,128)(2,1)S(1)}, u32[]{:S(2)}, u32[]{:S(2)}) %all-to-all-start.3) | async-done | bytes 229408 | tf_op jit(solution)/shard_map/all_to_all | solution.py:166
  253.9 0.9 reshape.203
  254.8 1.1 copy.107
  255.9 1.5 gather_fusion
  257.4 1.6 add_convert_fusion
  (80 shorter events, 2.3 us)
Async XLA Ops:
  6.5 175.2 %copy-start = (bf16[1,352,4096]{2,1,0:T(8,128)(2,1)S(1)}, bf16[1,352,4096]{2,1,0:T(8,128)(2,1)}, u32[]{:S(2)}) copy-start(bf16[1,352,4096]{2,1,0:T(8,128)(2,1)} %param.27) | copy-start | bytes 8650756
  11.9 10.3 %collective-permute-start = (bf16[128]{0:T(256)(128)(2,1)S(1)}, bf16[128]{0:T(256)(128)(2,1)S(1)}, u32[]{:S(2)}, u32[]{:S(2)}) collective-permute-start(bf16[128]{0:T(256)(128)(2,1)S(1)} %get-tuple-element.416), channel_id=1, source_target_pairs={{0,8},{8,16},{16,24},{24,32},{32,40},{40,48},{48,56},{56,64},{64,7... | collective-permute-start | bytes 776 | tf_op jit(solution)/shard_map/while/body/eval_jaxpr/ppermute | solution.py:20
  15.3 7.7 %collective-permute-start.1 = (bf16[128,2,128]{2,0,1:T(8,128)(2,1)S(1)}, bf16[128,2,128]{2,0,1:T(8,128)(2,1)S(1)}, u32[]{:S(2)}, u32[]{:S(2)}) collective-permute-start(bf16[128,2,128]{2,0,1:T(8,128)(2,1)S(1)} %get-tuple-element.414), channel_id=1, source_target_pairs={{0,8},{8,16},{16,24},{24,32},{32,40},{40,48},{48,56},{56,64},{64,7... | collective-permute-start | bytes 196616 | tf_op jit(solution)/shard_map/while/body/eval_jaxpr/ppermute | solution.py:20
  18.5 6.2 %collective-permute-start.2 = (bf16[128,2,128]{2,0,1:T(8,128)(2,1)S(1)}, bf16[128,2,128]{2,0,1:T(8,128)(2,1)S(1)}, u32[]{:S(2)}, u32[]{:S(2)}) collective-permute-start(bf16[128,2,128]{2,0,1:T(8,128)(2,1)S(1)} %get-tuple-element.415), channel_id=1, source_target_pairs={{0,8},{8,16},{16,24},{24,32},{32,40},{40,48},{48,56},{56,64},{64,7... | collective-permute-start | bytes 196616 | tf_op jit(solution)/shard_map/while/body/eval_jaxpr/ppermute | solution.py:20
  24.9 12.7 %collective-permute-start = (bf16[128]{0:T(256)(128)(2,1)S(1)}, bf16[128]{0:T(256)(128)(2,1)S(1)}, u32[]{:S(2)}, u32[]{:S(2)}) collective-permute-start(bf16[128]{0:T(256)(128)(2,1)S(1)} %get-tuple-element.416), channel_id=1, source_target_pairs={{0,8},{8,16},{16,24},{24,32},{32,40},{40,48},{48,56},{56,64},{64,7... | collective-permute-start | bytes 776 | tf_op jit(solution)/shard_map/while/body/eval_jaxpr/ppermute | solution.py:20
  28.6 9.7 %collective-permute-start.1 = (bf16[128,2,128]{2,0,1:T(8,128)(2,1)S(1)}, bf16[128,2,128]{2,0,1:T(8,128)(2,1)S(1)}, u32[]{:S(2)}, u32[]{:S(2)}) collective-permute-start(bf16[128,2,128]{2,0,1:T(8,128)(2,1)S(1)} %get-tuple-element.414), channel_id=1, source_target_pairs={{0,8},{8,16},{16,24},{24,32},{32,40},{40,48},{48,56},{56,64},{64,7... | collective-permute-start | bytes 196616 | tf_op jit(solution)/shard_map/while/body/eval_jaxpr/ppermute | solution.py:20
  32.0 7.4 %collective-permute-start.2 = (bf16[128,2,128]{2,0,1:T(8,128)(2,1)S(1)}, bf16[128,2,128]{2,0,1:T(8,128)(2,1)S(1)}, u32[]{:S(2)}, u32[]{:S(2)}) collective-permute-start(bf16[128,2,128]{2,0,1:T(8,128)(2,1)S(1)} %get-tuple-element.415), channel_id=1, source_target_pairs={{0,8},{8,16},{16,24},{24,32},{32,40},{40,48},{48,56},{56,64},{64,7... | collective-permute-start | bytes 196616 | tf_op jit(solution)/shard_map/while/body/eval_jaxpr/ppermute | solution.py:20
  39.7 10.4 %collective-permute-start = (bf16[128]{0:T(256)(128)(2,1)S(1)}, bf16[128]{0:T(256)(128)(2,1)S(1)}, u32[]{:S(2)}, u32[]{:S(2)}) collective-permute-start(bf16[128]{0:T(256)(128)(2,1)S(1)} %get-tuple-element.416), channel_id=1, source_target_pairs={{0,8},{8,16},{16,24},{24,32},{32,40},{40,48},{48,56},{56,64},{64,7... | collective-permute-start | bytes 776 | tf_op jit(solution)/shard_map/while/body/eval_jaxpr/ppermute | solution.py:20
  44.0 6.9 %collective-permute-start.1 = (bf16[128,2,128]{2,0,1:T(8,128)(2,1)S(1)}, bf16[128,2,128]{2,0,1:T(8,128)(2,1)S(1)}, u32[]{:S(2)}, u32[]{:S(2)}) collective-permute-start(bf16[128,2,128]{2,0,1:T(8,128)(2,1)S(1)} %get-tuple-element.414), channel_id=1, source_target_pairs={{0,8},{8,16},{16,24},{24,32},{32,40},{40,48},{48,56},{56,64},{64,7... | collective-permute-start | bytes 196616 | tf_op jit(solution)/shard_map/while/body/eval_jaxpr/ppermute | solution.py:20
  45.9 6.2 %collective-permute-start.2 = (bf16[128,2,128]{2,0,1:T(8,128)(2,1)S(1)}, bf16[128,2,128]{2,0,1:T(8,128)(2,1)S(1)}, u32[]{:S(2)}, u32[]{:S(2)}) collective-permute-start(bf16[128,2,128]{2,0,1:T(8,128)(2,1)S(1)} %get-tuple-element.415), channel_id=1, source_target_pairs={{0,8},{8,16},{16,24},{24,32},{32,40},{40,48},{48,56},{56,64},{64,7... | collective-permute-start | bytes 196616 | tf_op jit(solution)/shard_map/while/body/eval_jaxpr/ppermute | solution.py:20
  52.4 14.0 %collective-permute-start = (bf16[128]{0:T(256)(128)(2,1)S(1)}, bf16[128]{0:T(256)(128)(2,1)S(1)}, u32[]{:S(2)}, u32[]{:S(2)}) collective-permute-start(bf16[128]{0:T(256)(128)(2,1)S(1)} %get-tuple-element.416), channel_id=1, source_target_pairs={{0,8},{8,16},{16,24},{24,32},{32,40},{40,48},{48,56},{56,64},{64,7... | collective-permute-start | bytes 776 | tf_op jit(solution)/shard_map/while/body/eval_jaxpr/ppermute | solution.py:20
  56.5 10.6 %collective-permute-start.1 = (bf16[128,2,128]{2,0,1:T(8,128)(2,1)S(1)}, bf16[128,2,128]{2,0,1:T(8,128)(2,1)S(1)}, u32[]{:S(2)}, u32[]{:S(2)}) collective-permute-start(bf16[128,2,128]{2,0,1:T(8,128)(2,1)S(1)} %get-tuple-element.414), channel_id=1, source_target_pairs={{0,8},{8,16},{16,24},{24,32},{32,40},{40,48},{48,56},{56,64},{64,7... | collective-permute-start | bytes 196616 | tf_op jit(solution)/shard_map/while/body/eval_jaxpr/ppermute | solution.py:20
  59.9 8.3 %collective-permute-start.2 = (bf16[128,2,128]{2,0,1:T(8,128)(2,1)S(1)}, bf16[128,2,128]{2,0,1:T(8,128)(2,1)S(1)}, u32[]{:S(2)}, u32[]{:S(2)}) collective-permute-start(bf16[128,2,128]{2,0,1:T(8,128)(2,1)S(1)} %get-tuple-element.415), channel_id=1, source_target_pairs={{0,8},{8,16},{16,24},{24,32},{32,40},{40,48},{48,56},{56,64},{64,7... | collective-permute-start | bytes 196616 | tf_op jit(solution)/shard_map/while/body/eval_jaxpr/ppermute | solution.py:20
  70.7 9.8 %copy-start.6 = (s32[128]{0:T(128)S(1)}, s32[128]{0:T(128)}, u32[]{:S(2)}) copy-start(s32[128]{0:T(128)} %param.24) | copy-start | bytes 1540
  70.7 9.8 %copy-start.7 = (s32[128]{0:T(128)S(1)}, s32[128]{0:T(128)}, u32[]{:S(2)}) copy-start(s32[128]{0:T(128)} %param.23) | copy-start | bytes 1540
  71.8 39.3 %copy-start.2 = (bf16[128,512]{1,0:T(8,128)(2,1)S(1)}, bf16[128,512]{1,0:T(8,128)(2,1)}, u32[]{:S(2)}) copy-start(bf16[128,512]{1,0:T(8,128)(2,1)} %param.19) | copy-start | bytes 393220
  71.8 51.0 %copy-start.4 = (f32[512]{0:T(512)S(1)}, f32[512]{0:T(512)}, u32[]{:S(2)}) copy-start(f32[512]{0:T(512)} %param.21) | copy-start | bytes 6148
  71.8 37.9 %all-to-all-start = ((bf16[8,128,512]{2,1,0:T(8,128)(2,1)}), bf16[8,128,512]{2,1,0:T(8,128)(2,1)}, u32[]{:S(2)}, u32[]{:S(2)}) async-start(bf16[8,128,512]{2,1,0:T(8,128)(2,1)} %bitcast.76), calls=%async_computation | async-start | bytes 2097152 | tf_op jit(solution)/shard_map/all_to_all | solution.py:31
  111.9 10.9 %all-to-all-start.1 = ((f32[8,1,128]{2,1,0:T(1,128)}), f32[8,1,128]{2,1,0:T(1,128)S(1)}, u32[]{:S(2)}, u32[]{:S(2)}) async-start(f32[8,1,128]{2,1,0:T(1,128)} %broadcast_in_dim.92), calls=%async_computation.1 | async-start | bytes 8192 | tf_op jit(solution)/shard_map/all_to_all | solution.py:37
  115.2 59.8 %all-gather.3.cloned.1.call-start = ((), (), s32[]{:S(2)}) async-start(), calls=%async_computation.6 | async-start | bytes 2752512 | tf_op jit(solution)/shard_map/all_gather | solution.py:54
  162.8 69.4 %reduce-scatter.2.cloned.1.call-start = ((), (), s32[]{:S(2)}) async-start(), calls=%async_computation.5 | async-start | bytes 2064384 | tf_op jit(solution)/shard_map/reduce_scatter | solution.py:163
  176.7 2.5 copy-start.5
  177.0 4.2 %copy-start.1 = (bf16[28,8,8,512]{3,1,2,0:T(8,128)(2,1)}, bf16[28,8,8,512]{3,1,2,0:T(8,128)(2,1)S(1)}, u32[]{:S(2)}) copy-start(bf16[28,8,8,512]{3,1,2,0:T(8,128)(2,1)S(1)} %copy.101) | copy-start | bytes 5505028
  179.2 1.9 copy-start.3
  238.4 15.5 %all-to-all-start.3 = ((bf16[32,2,1792]{2,1,0:T(2,128)(2,1)}), bf16[32,2,1792]{2,1,0:T(2,128)(2,1)S(1)}, u32[]{:S(2)}, u32[]{:S(2)}) async-start(bf16[32,2,1792]{2,1,0:T(2,128)(2,1)} %reshape.202), calls=%async_computation.4 | async-start | bytes 458752 | tf_op jit(solution)/shard_map/all_to_all | solution.py:166
Sparse Core Ops, SparseCore 0:
  162.9 12.1 all-gather.2
  188.0 44.1 reduce-scatter.1
where the time goes:
time: 267 us; the launch traced here: 266 us
  waiting for transfers between devices  105 us (39%)
  starting transfers between devices  66.5 us (25%)
  blocking collectives  36.9 us (14%)
  local copies, waits for them, and re-layouts  18 us (7%)
  between operations  13.7 us (5%)
  matrix products  12.9 us (5%)
  other arithmetic  12.6 us (5%)
    ppermute x12, starting transfers between devices, passed_along(): lax.ppermute(value, axis, [(source, source + steps) for source in range(l...  47.2 us
    reduce_scatter x1, waiting for transfers between devices, local(): lax.psum_scatter(partial_value.astype(jnp.bfloat16), EXP, scatter_dimensi...  44.3 us
    all_to_all x1, waiting for transfers between devices, sent_and_summed(): tiles = lax.all_to_all(split_up(array, dim, length), axis, 0, 0, tiled=True)  28.9 us
    all_gather x1, blocking collectives, stacked_from(): tiles = lax.all_gather(tiles, axes[k])  20.1 us
    all_to_all x1, blocking collectives, local(): lax.all_to_all(outgoing.reshape(EXPERTS, CAPACITY, normed.shape[1]), 'seq...  16.9 us
    all_gather x1, waiting for transfers between devices, stacked_from(): tiles = lax.all_gather(tiles, axes[k])  12.2 us
    unnamed x24, local copies, waits for them, and re-layouts  8.64 us
    all_to_all x1, starting transfers between devices, sent_and_summed(): tiles = lax.all_to_all(split_up(array, dim, length), axis, 0, 0, tiled=True)  8.59 us
  transfers between devices with their start and end apart: 17, of which 9 were waited for; matrix products, arithmetic and copies ran while one was open for 2% of the time, Pallas kernels for 0%

commit v1 on v0

--- a/solution.py
+++ b/solution.py
@@ -143,13 +143,12 @@
     outgoing = (
         jnp.zeros((EXPERTS * CAPACITY, normed.shape[1]), jnp.bfloat16).at[slot_index].set(normed)
     )
-    sliced = lax.all_to_all(
-        outgoing.reshape(EXPERTS, CAPACITY, normed.shape[1]),
-        "seq",
-        split_axis=0,
-        concat_axis=1,
-        tiled=True,
-    )
+    incoming_x = outgoing.reshape(EXPERTS, CAPACITY, normed.shape[1])
+    spare = lax.psum(1, axis_name="seq")
+    all_values = jnp.split(incoming_x, spare, 0)
+    e_next = jnp.stack(all_values, 0)
+    big = lax.all_to_all(e_next, split_axis=0, concat_axis=0, axis_name="seq")
+    sliced = jnp.concatenate(big, 1)
     arrived = gather_axes(sliced, EXP, (0, 1), 2)
     gate_sum = jnp.einsum("erd,edf->erf", arrived, gate_weight, preferred_element_type=jnp.float32)
     up_sum = jnp.einsum("erd,edf->erf", arrived, up_weight, preferred_element_type=jnp.float32)

time: 267 us -> 266 us (level)
    unnamed x24 -> x55, local copies, waits for them, and re-layouts: 8.64 us -> 8.85 us
where the time goes in v1:
time: 266 us; the launch traced here: 265 us
  waiting for transfers between devices  105 us (39%)
  starting transfers between devices  66.6 us (25%)
  blocking collectives  36.7 us (14%)
  local copies, waits for them, and re-layouts  17.4 us (7%)
  between operations  13.9 us (5%)
  matrix products  12.9 us (5%)
  other arithmetic  12.6 us (5%)
    ppermute x12, starting transfers between devices, passed_along(): lax.ppermute(value, axis, [(source, source + steps) for source in range(l...  47.2 us
    reduce_scatter x1, waiting for transfers between devices, local(): lax.psum_scatter(partial_value.astype(jnp.bfloat16), EXP, scatter_dimensi...  44.3 us
    all_to_all x1, waiting for transfers between devices, sent_and_summed(): tiles = lax.all_to_all(split_up(array, dim, length), axis, 0, 0, tiled=True)  28.9 us
    all_gather x1, blocking collectives, stacked_from(): tiles = lax.all_gather(tiles, axes[k])  20.1 us
    all_to_all x1, blocking collectives, local(): big = lax.all_to_all(e_next, split_axis=0, concat_axis=0, axis_name='seq')  16.7 us
    all_gather x1, waiting for transfers between devices, stacked_from(): tiles = lax.all_gather(tiles, axes[k])  12.2 us
    unnamed x55, local copies, waits for them, and re-layouts  8.85 us
    all_to_all x1, starting transfers between devices, sent_and_summed(): tiles = lax.all_to_all(split_up(array, dim, length), axis, 0, 0, tiled=True)  8.59 us
  transfers between devices with their start and end apart: 17, of which 9 were waited for; matrix products, arithmetic and copies ran while one was open for 2% of the time, Pallas kernels for 0%

profile of v1, /device:TPU:2, one launch (start us, length us, event | category | flops | bytes accessed | tf_op | source)
XLA Modules:
  0.0 265.3 jit_solution(10153336820321099183)
XLA Ops:
  6.5 0.9 fusion.41
  7.4 0.7 convert_element_type.62
  8.1 0.9 copy.109
  9.1 1.0 copy.110
  10.3 0.2 fusion.44
  10.6 1.0 copy.113
  11.7 0.2 convolution_add_fusion.1
  11.9 56.5 %while.25 = (s32[]{:T(128)}, f32[2,128]{1,0:T(2,128)S(1)}, f32[2,128]{1,0:T(2,128)S(1)}, f32[2,128,128]{2,1,0:T(8,128)S(1)}, bf16[128,2,128]{2,0,1:T(8,128)(2,1)...) while((s32[]{:T(128)}, f32[2,128]{1,0:T(2,128)S(1)}, ...), condition=%wide.region_5.6_spmd, body=%wide.region_2.5_spmd.sunk | while | flops 17171076 | bytes 1723927 | solution.py:127
  11.9 3.4 %collective-permute-start = (bf16[128]{0:T(256)(128)(2,1)S(1)}, bf16[128]{0:T(256)(128)(2,1)S(1)}, u32[]{:S(2)}, u32[]{:S(2)}) collective-permute-start(bf16[128]{0:T(256)(128)(2,1)S(1)} %get-tuple-element.416), channel_id=1, source_target_pairs={{0,8},{8,16},{16,24},{24,32},{32,40},{40,48},{48,56},{56,64},{64,7... | collective-permute-start | bytes 776 | tf_op jit(solution)/shard_map/while/body/eval_jaxpr/ppermute | solution.py:20
  15.3 3.1 %collective-permute-start.1 = (bf16[128,2,128]{2,0,1:T(8,128)(2,1)S(1)}, bf16[128,2,128]{2,0,1:T(8,128)(2,1)S(1)}, u32[]{:S(2)}, u32[]{:S(2)}) collective-permute-start(bf16[128,2,128]{2,0,1:T(8,128)(2,1)S(1)} %get-tuple-element.414), channel_id=1, source_target_pairs={{0,8},{8,16},{16,24},{24,32},{32,40},{40,48},{48,56},{56,64},{64,7... | collective-permute-start | bytes 196616 | tf_op jit(solution)/shard_map/while/body/eval_jaxpr/ppermute | solution.py:20
  18.5 3.7 %collective-permute-start.2 = (bf16[128,2,128]{2,0,1:T(8,128)(2,1)S(1)}, bf16[128,2,128]{2,0,1:T(8,128)(2,1)S(1)}, u32[]{:S(2)}, u32[]{:S(2)}) collective-permute-start(bf16[128,2,128]{2,0,1:T(8,128)(2,1)S(1)} %get-tuple-element.415), channel_id=1, source_target_pairs={{0,8},{8,16},{16,24},{24,32},{32,40},{40,48},{48,56},{56,64},{64,7... | collective-permute-start | bytes 196616 | tf_op jit(solution)/shard_map/while/body/eval_jaxpr/ppermute | solution.py:20
  22.2 0.7 compare_and_fusion.2
  23.0 0.2 select_reduce_fusion.3
  23.3 1.3 collective-permute-done.2
  24.6 0.2 convolution_add_fusion.3
  24.9 3.7 %collective-permute-start = (bf16[128]{0:T(256)(128)(2,1)S(1)}, bf16[128]{0:T(256)(128)(2,1)S(1)}, u32[]{:S(2)}, u32[]{:S(2)}) collective-permute-start(bf16[128]{0:T(256)(128)(2,1)S(1)} %get-tuple-element.416), channel_id=1, source_target_pairs={{0,8},{8,16},{16,24},{24,32},{32,40},{40,48},{48,56},{56,64},{64,7... | collective-permute-start | bytes 776 | tf_op jit(solution)/shard_map/while/body/eval_jaxpr/ppermute | solution.py:20
  28.6 3.4 %collective-permute-start.1 = (bf16[128,2,128]{2,0,1:T(8,128)(2,1)S(1)}, bf16[128,2,128]{2,0,1:T(8,128)(2,1)S(1)}, u32[]{:S(2)}, u32[]{:S(2)}) collective-permute-start(bf16[128,2,128]{2,0,1:T(8,128)(2,1)S(1)} %get-tuple-element.414), channel_id=1, source_target_pairs={{0,8},{8,16},{16,24},{24,32},{32,40},{40,48},{48,56},{56,64},{64,7... | collective-permute-start | bytes 196616 | tf_op jit(solution)/shard_map/while/body/eval_jaxpr/ppermute | solution.py:20
  32.0 5.5 %collective-permute-start.2 = (bf16[128,2,128]{2,0,1:T(8,128)(2,1)S(1)}, bf16[128,2,128]{2,0,1:T(8,128)(2,1)S(1)}, u32[]{:S(2)}, u32[]{:S(2)}) collective-permute-start(bf16[128,2,128]{2,0,1:T(8,128)(2,1)S(1)} %get-tuple-element.415), channel_id=1, source_target_pairs={{0,8},{8,16},{16,24},{24,32},{32,40},{40,48},{48,56},{56,64},{64,7... | collective-permute-start | bytes 196616 | tf_op jit(solution)/shard_map/while/body/eval_jaxpr/ppermute | solution.py:20
  37.6 0.7 compare_and_fusion.2
  38.7 0.8 collective-permute-done.2
  39.5 0.2 convolution_add_fusion.3
  39.7 4.3 %collective-permute-start = (bf16[128]{0:T(256)(128)(2,1)S(1)}, bf16[128]{0:T(256)(128)(2,1)S(1)}, u32[]{:S(2)}, u32[]{:S(2)}) collective-permute-start(bf16[128]{0:T(256)(128)(2,1)S(1)} %get-tuple-element.416), channel_id=1, source_target_pairs={{0,8},{8,16},{16,24},{24,32},{32,40},{40,48},{48,56},{56,64},{64,7... | collective-permute-start | bytes 776 | tf_op jit(solution)/shard_map/while/body/eval_jaxpr/ppermute | solution.py:20
  44.0 1.9 collective-permute-start.1
  45.9 4.1 %collective-permute-start.2 = (bf16[128,2,128]{2,0,1:T(8,128)(2,1)S(1)}, bf16[128,2,128]{2,0,1:T(8,128)(2,1)S(1)}, u32[]{:S(2)}, u32[]{:S(2)}) collective-permute-start(bf16[128,2,128]{2,0,1:T(8,128)(2,1)S(1)} %get-tuple-element.415), channel_id=1, source_target_pairs={{0,8},{8,16},{16,24},{24,32},{32,40},{40,48},{48,56},{56,64},{64,7... | collective-permute-start | bytes 196616 | tf_op jit(solution)/shard_map/while/body/eval_jaxpr/ppermute | solution.py:20
  50.1 0.7 compare_and_fusion.2
  51.2 0.9 collective-permute-done.2
  52.1 0.2 convolution_add_fusion.3
  52.4 4.1 %collective-permute-start = (bf16[128]{0:T(256)(128)(2,1)S(1)}, bf16[128]{0:T(256)(128)(2,1)S(1)}, u32[]{:S(2)}, u32[]{:S(2)}) collective-permute-start(bf16[128]{0:T(256)(128)(2,1)S(1)} %get-tuple-element.416), channel_id=1, source_target_pairs={{0,8},{8,16},{16,24},{24,32},{32,40},{40,48},{48,56},{56,64},{64,7... | collective-permute-start | bytes 776 | tf_op jit(solution)/shard_map/while/body/eval_jaxpr/ppermute | solution.py:20
  56.5 3.4 %collective-permute-start.1 = (bf16[128,2,128]{2,0,1:T(8,128)(2,1)S(1)}, bf16[128,2,128]{2,0,1:T(8,128)(2,1)S(1)}, u32[]{:S(2)}, u32[]{:S(2)}) collective-permute-start(bf16[128,2,128]{2,0,1:T(8,128)(2,1)S(1)} %get-tuple-element.414), channel_id=1, source_target_pairs={{0,8},{8,16},{16,24},{24,32},{32,40},{40,48},{48,56},{56,64},{64,7... | collective-permute-start | bytes 196616 | tf_op jit(solution)/shard_map/while/body/eval_jaxpr/ppermute | solution.py:20
  59.9 6.4 %collective-permute-start.2 = (bf16[128,2,128]{2,0,1:T(8,128)(2,1)S(1)}, bf16[128,2,128]{2,0,1:T(8,128)(2,1)S(1)}, u32[]{:S(2)}, u32[]{:S(2)}) collective-permute-start(bf16[128,2,128]{2,0,1:T(8,128)(2,1)S(1)} %get-tuple-element.415), channel_id=1, source_target_pairs={{0,8},{8,16},{16,24},{24,32},{32,40},{40,48},{48,56},{56,64},{64,7... | collective-permute-start | bytes 196616 | tf_op jit(solution)/shard_map/while/body/eval_jaxpr/ppermute | solution.py:20
  66.3 0.7 compare_and_fusion.2
  67.1 0.2 select_reduce_fusion.3
  67.4 0.8 collective-permute-done.2
  68.2 0.2 convolution_add_fusion.3
  68.6 2.1 convolution_convert_fusion.1
  70.7 1.1 copy.137
  71.8 8.6 %all-to-all-start = ((bf16[8,128,512]{2,1,0:T(8,128)(2,1)}), bf16[8,128,512]{2,1,0:T(8,128)(2,1)}, u32[]{:S(2)}, u32[]{:S(2)}) async-start(bf16[8,128,512]{2,1,0:T(8,128)(2,1)} %bitcast.204), calls=%async_computation | async-start | bytes 2097152 | tf_op jit(solution)/shard_map/all_to_all | solution.py:31
  80.9 28.9 %all-to-all-done = bf16[8,128,512]{2,1,0:T(8,128)(2,1)} async-done(((bf16[8,128,512]{2,1,0:T(8,128)(2,1)}), bf16[8,128,512]{2,1,0:T(8,128)(2,1)}, u32[]{:S(2)}, u32[]{:S(2)}) %all-to-all-start) | async-done | bytes 1048608 | tf_op jit(solution)/shard_map/all_to_all | solution.py:31
  109.8 1.4 convert_reduce_fusion
  111.3 0.6 broadcast_in_dim.92
  111.9 3.3 %all-to-all-start.1 = ((f32[8,1,128]{2,1,0:T(1,128)}), f32[8,1,128]{2,1,0:T(1,128)S(1)}, u32[]{:S(2)}, u32[]{:S(2)}) async-start(f32[8,1,128]{2,1,0:T(1,128)} %broadcast_in_dim.92), calls=%async_computation.1 | async-start | bytes 8192 | tf_op jit(solution)/shard_map/all_to_all | solution.py:37
  115.3 7.5 %all-to-all-done.1 = f32[8,1,128]{2,1,0:T(1,128)S(1)} async-done(((f32[8,1,128]{2,1,0:T(1,128)}), f32[8,1,128]{2,1,0:T(1,128)S(1)}, u32[]{:S(2)}, u32[]{:S(2)}) %all-to-all-start.1) | async-done | bytes 4128 | tf_op jit(solution)/shard_map/all_to_all | solution.py:37
  122.8 1.2 scatter_custom_fusion
  124.4 16.7 %all_to_all.25 = bf16[32,1,7,512]{3,2,1,0:T(8,128)(2,1)} all-to-all(bf16[32,1,7,512]{3,2,1,0:T(8,128)(2,1)S(1)} %constant_dynamic-update-slice_fusion), channel_id=1, replica_groups=mesh['seq'=32,'exp_0'=4,'exp_1'=2] {'seq'}, dimensions={0} | all-to-all | bytes 458752 | tf_op jit(solution)/shard_map/all_to_all | solution.py:150
  141.1 1.0 all_gather_reshape.3
  142.2 20.1 %all_gather.9 = bf16[4,1,224,512]{3,2,1,0:T(8,128)(2,1)} all-gather(bf16[1,1,224,512]{3,2,1,0:T(8,128)(2,1)S(1)} %all_gather_reshape.3), channel_id=1, replica_groups=mesh['seq'=32,'exp_0'=4,'exp_1'=2] {'exp_0'}, dimensions={0}, use_global_device_ids=true | all-gather | bytes 1146880 | tf_op jit(solution)/shard_map/all_gather | solution.py:54
  162.3 12.2 %all-gather.3.cloned.1.call-done = bf16[8,1,224,512]{3,2,1,0:T(8,128)(2,1)} async-done(((bf16[4,1,224,512]{3,2,1,0:T(8,128)(2,1)}), bf16[8,1,224,512]{3,2,1,0:T(8,128)(2,1)}) %all-gather.3.cloned.1.call-update) | async-done | bytes 1835024 | tf_op jit(solution)/shard_map/all_gather | solution.py:54
  174.5 1.7 copy.122
  176.2 0.2 copy.132
  176.5 2.2 copy-done.5
  178.7 1.9 fusion.11
  180.6 0.6 fusion.45
  181.2 6.1 %fusion.7 = bf16[1,224,4096]{2,1,0:T(8,128)(2,1)} fusion(bf16[1,352,4096]{2,1,0:T(8,128)(2,1)S(1)} %copy-done, bf16[224,4096]{1,0:T(8,128)(2,1)} %bitcast.200, bf16[1,4096,352]{1,2,0:T(8,128)(2,1)} %param.26, f32[224,352]{1,0:T(8,128)} %fusion.11, f32[224]{0:T(256)S(1)} %add_divide_fusion), kind=kOutput, calls=%fused_computation.16 | convolution fusion | flops 1293315072 | bytes 9753472 | tf_op jit(solution)/shard_map/erf,efd->erd/dot_general | solution.py:159
  187.3 44.3 %reduce-scatter.2.cloned.1.call-done = bf16[1,224,512]{2,1,0:T(8,128)(2,1)} async-done(((bf16[1,224,4096]{2,1,0:T(8,128)(2,1)}), bf16[1,224,512]{2,1,0:T(8,128)(2,1)}) %reduce-scatter.2.cloned.1.call-update) | async-done | bytes 229392 | tf_op jit(solution)/shard_map/reduce_scatter | solution.py:162
  231.6 2.1 copy.139
  233.7 0.5 broadcast.146
  234.2 2.9 %reduce.1 = bf16[224,512]{1,0:T(8,128)(2,1)S(1)} reduce(bf16[224,1,512]{2,1,0:T(2,128)(2,1)} %bitcast.206, bf16[]{:T(256)} %broadcast.146), dimensions={1}, to_apply=%bitcast.191.reduce_sub_computation | reduce | bytes 458754
  237.1 0.8 reshape.259
  237.9 7.4 %all-to-all-start.3 = ((bf16[32,2,1792]{2,1,0:T(2,128)(2,1)}), bf16[32,2,1792]{2,1,0:T(2,128)(2,1)S(1)}, u32[]{:S(2)}, u32[]{:S(2)}) async-start(bf16[32,2,1792]{2,1,0:T(2,128)(2,1)} %reshape.259), calls=%async_computation.4 | async-start | bytes 458752 | tf_op jit(solution)/shard_map/all_to_all | solution.py:165
  245.4 8.0 %all-to-all-done.3 = bf16[32,2,1792]{2,1,0:T(2,128)(2,1)S(1)} async-done(((bf16[32,2,1792]{2,1,0:T(2,128)(2,1)}), bf16[32,2,1792]{2,1,0:T(2,128)(2,1)S(1)}, u32[]{:S(2)}, u32[]{:S(2)}) %all-to-all-start.3) | async-done | bytes 229408 | tf_op jit(solution)/shard_map/all_to_all | solution.py:165
  253.4 0.9 reshape.260
  254.3 1.1 copy.138
  255.4 1.5 gather_fusion
  256.9 1.6 add_convert_fusion
  (111 shorter events, 2.3 us)
Async XLA Ops:
  6.5 174.7 %copy-start = (bf16[1,352,4096]{2,1,0:T(8,128)(2,1)S(1)}, bf16[1,352,4096]{2,1,0:T(8,128)(2,1)}, u32[]{:S(2)}) copy-start(bf16[1,352,4096]{2,1,0:T(8,128)(2,1)} %param.27) | copy-start | bytes 8650756
  11.9 10.3 %collective-permute-start = (bf16[128]{0:T(256)(128)(2,1)S(1)}, bf16[128]{0:T(256)(128)(2,1)S(1)}, u32[]{:S(2)}, u32[]{:S(2)}) collective-permute-start(bf16[128]{0:T(256)(128)(2,1)S(1)} %get-tuple-element.416), channel_id=1, source_target_pairs={{0,8},{8,16},{16,24},{24,32},{32,40},{40,48},{48,56},{56,64},{64,7... | collective-permute-start | bytes 776 | tf_op jit(solution)/shard_map/while/body/eval_jaxpr/ppermute | solution.py:20
  15.3 7.7 %collective-permute-start.1 = (bf16[128,2,128]{2,0,1:T(8,128)(2,1)S(1)}, bf16[128,2,128]{2,0,1:T(8,128)(2,1)S(1)}, u32[]{:S(2)}, u32[]{:S(2)}) collective-permute-start(bf16[128,2,128]{2,0,1:T(8,128)(2,1)S(1)} %get-tuple-element.414), channel_id=1, source_target_pairs={{0,8},{8,16},{16,24},{24,32},{32,40},{40,48},{48,56},{56,64},{64,7... | collective-permute-start | bytes 196616 | tf_op jit(solution)/shard_map/while/body/eval_jaxpr/ppermute | solution.py:20
  18.5 6.2 %collective-permute-start.2 = (bf16[128,2,128]{2,0,1:T(8,128)(2,1)S(1)}, bf16[128,2,128]{2,0,1:T(8,128)(2,1)S(1)}, u32[]{:S(2)}, u32[]{:S(2)}) collective-permute-start(bf16[128,2,128]{2,0,1:T(8,128)(2,1)S(1)} %get-tuple-element.415), channel_id=1, source_target_pairs={{0,8},{8,16},{16,24},{24,32},{32,40},{40,48},{48,56},{56,64},{64,7... | collective-permute-start | bytes 196616 | tf_op jit(solution)/shard_map/while/body/eval_jaxpr/ppermute | solution.py:20
  24.9 12.7 %collective-permute-start = (bf16[128]{0:T(256)(128)(2,1)S(1)}, bf16[128]{0:T(256)(128)(2,1)S(1)}, u32[]{:S(2)}, u32[]{:S(2)}) collective-permute-start(bf16[128]{0:T(256)(128)(2,1)S(1)} %get-tuple-element.416), channel_id=1, source_target_pairs={{0,8},{8,16},{16,24},{24,32},{32,40},{40,48},{48,56},{56,64},{64,7... | collective-permute-start | bytes 776 | tf_op jit(solution)/shard_map/while/body/eval_jaxpr/ppermute | solution.py:20
  28.6 9.7 %collective-permute-start.1 = (bf16[128,2,128]{2,0,1:T(8,128)(2,1)S(1)}, bf16[128,2,128]{2,0,1:T(8,128)(2,1)S(1)}, u32[]{:S(2)}, u32[]{:S(2)}) collective-permute-start(bf16[128,2,128]{2,0,1:T(8,128)(2,1)S(1)} %get-tuple-element.414), channel_id=1, source_target_pairs={{0,8},{8,16},{16,24},{24,32},{32,40},{40,48},{48,56},{56,64},{64,7... | collective-permute-start | bytes 196616 | tf_op jit(solution)/shard_map/while/body/eval_jaxpr/ppermute | solution.py:20
  32.0 7.4 %collective-permute-start.2 = (bf16[128,2,128]{2,0,1:T(8,128)(2,1)S(1)}, bf16[128,2,128]{2,0,1:T(8,128)(2,1)S(1)}, u32[]{:S(2)}, u32[]{:S(2)}) collective-permute-start(bf16[128,2,128]{2,0,1:T(8,128)(2,1)S(1)} %get-tuple-element.415), channel_id=1, source_target_pairs={{0,8},{8,16},{16,24},{24,32},{32,40},{40,48},{48,56},{56,64},{64,7... | collective-permute-start | bytes 196616 | tf_op jit(solution)/shard_map/while/body/eval_jaxpr/ppermute | solution.py:20
  39.7 10.4 %collective-permute-start = (bf16[128]{0:T(256)(128)(2,1)S(1)}, bf16[128]{0:T(256)(128)(2,1)S(1)}, u32[]{:S(2)}, u32[]{:S(2)}) collective-permute-start(bf16[128]{0:T(256)(128)(2,1)S(1)} %get-tuple-element.416), channel_id=1, source_target_pairs={{0,8},{8,16},{16,24},{24,32},{32,40},{40,48},{48,56},{56,64},{64,7... | collective-permute-start | bytes 776 | tf_op jit(solution)/shard_map/while/body/eval_jaxpr/ppermute | solution.py:20
  44.0 6.9 %collective-permute-start.1 = (bf16[128,2,128]{2,0,1:T(8,128)(2,1)S(1)}, bf16[128,2,128]{2,0,1:T(8,128)(2,1)S(1)}, u32[]{:S(2)}, u32[]{:S(2)}) collective-permute-start(bf16[128,2,128]{2,0,1:T(8,128)(2,1)S(1)} %get-tuple-element.414), channel_id=1, source_target_pairs={{0,8},{8,16},{16,24},{24,32},{32,40},{40,48},{48,56},{56,64},{64,7... | collective-permute-start | bytes 196616 | tf_op jit(solution)/shard_map/while/body/eval_jaxpr/ppermute | solution.py:20
  45.9 6.2 %collective-permute-start.2 = (bf16[128,2,128]{2,0,1:T(8,128)(2,1)S(1)}, bf16[128,2,128]{2,0,1:T(8,128)(2,1)S(1)}, u32[]{:S(2)}, u32[]{:S(2)}) collective-permute-start(bf16[128,2,128]{2,0,1:T(8,128)(2,1)S(1)} %get-tuple-element.415), channel_id=1, source_target_pairs={{0,8},{8,16},{16,24},{24,32},{32,40},{40,48},{48,56},{56,64},{64,7... | collective-permute-start | bytes 196616 | tf_op jit(solution)/shard_map/while/body/eval_jaxpr/ppermute | solution.py:20
  52.4 14.0 %collective-permute-start = (bf16[128]{0:T(256)(128)(2,1)S(1)}, bf16[128]{0:T(256)(128)(2,1)S(1)}, u32[]{:S(2)}, u32[]{:S(2)}) collective-permute-start(bf16[128]{0:T(256)(128)(2,1)S(1)} %get-tuple-element.416), channel_id=1, source_target_pairs={{0,8},{8,16},{16,24},{24,32},{32,40},{40,48},{48,56},{56,64},{64,7... | collective-permute-start | bytes 776 | tf_op jit(solution)/shard_map/while/body/eval_jaxpr/ppermute | solution.py:20
  56.5 10.6 %collective-permute-start.1 = (bf16[128,2,128]{2,0,1:T(8,128)(2,1)S(1)}, bf16[128,2,128]{2,0,1:T(8,128)(2,1)S(1)}, u32[]{:S(2)}, u32[]{:S(2)}) collective-permute-start(bf16[128,2,128]{2,0,1:T(8,128)(2,1)S(1)} %get-tuple-element.414), channel_id=1, source_target_pairs={{0,8},{8,16},{16,24},{24,32},{32,40},{40,48},{48,56},{56,64},{64,7... | collective-permute-start | bytes 196616 | tf_op jit(solution)/shard_map/while/body/eval_jaxpr/ppermute | solution.py:20
  59.9 8.3 %collective-permute-start.2 = (bf16[128,2,128]{2,0,1:T(8,128)(2,1)S(1)}, bf16[128,2,128]{2,0,1:T(8,128)(2,1)S(1)}, u32[]{:S(2)}, u32[]{:S(2)}) collective-permute-start(bf16[128,2,128]{2,0,1:T(8,128)(2,1)S(1)} %get-tuple-element.415), channel_id=1, source_target_pairs={{0,8},{8,16},{16,24},{24,32},{32,40},{40,48},{48,56},{56,64},{64,7... | collective-permute-start | bytes 196616 | tf_op jit(solution)/shard_map/while/body/eval_jaxpr/ppermute | solution.py:20
  70.7 9.8 %copy-start.6 = (s32[128]{0:T(128)S(1)}, s32[128]{0:T(128)}, u32[]{:S(2)}) copy-start(s32[128]{0:T(128)} %param.24) | copy-start | bytes 1540
  70.7 9.8 %copy-start.7 = (s32[128]{0:T(128)S(1)}, s32[128]{0:T(128)}, u32[]{:S(2)}) copy-start(s32[128]{0:T(128)} %param.23) | copy-start | bytes 1540
  71.8 39.3 %copy-start.2 = (bf16[128,512]{1,0:T(8,128)(2,1)S(1)}, bf16[128,512]{1,0:T(8,128)(2,1)}, u32[]{:S(2)}) copy-start(bf16[128,512]{1,0:T(8,128)(2,1)} %param.19) | copy-start | bytes 393220
  71.8 51.0 %copy-start.4 = (f32[512]{0:T(512)S(1)}, f32[512]{0:T(512)}, u32[]{:S(2)}) copy-start(f32[512]{0:T(512)} %param.21) | copy-start | bytes 6148
  71.8 37.9 %all-to-all-start = ((bf16[8,128,512]{2,1,0:T(8,128)(2,1)}), bf16[8,128,512]{2,1,0:T(8,128)(2,1)}, u32[]{:S(2)}, u32[]{:S(2)}) async-start(bf16[8,128,512]{2,1,0:T(8,128)(2,1)} %bitcast.204), calls=%async_computation | async-start | bytes 2097152 | tf_op jit(solution)/shard_map/all_to_all | solution.py:31
  111.9 10.9 %all-to-all-start.1 = ((f32[8,1,128]{2,1,0:T(1,128)}), f32[8,1,128]{2,1,0:T(1,128)S(1)}, u32[]{:S(2)}, u32[]{:S(2)}) async-start(f32[8,1,128]{2,1,0:T(1,128)} %broadcast_in_dim.92), calls=%async_computation.1 | async-start | bytes 8192 | tf_op jit(solution)/shard_map/all_to_all | solution.py:37
  115.2 59.3 %all-gather.3.cloned.1.call-start = ((), (), s32[]{:S(2)}) async-start(), calls=%async_computation.6 | async-start | bytes 2752512 | tf_op jit(solution)/shard_map/all_gather | solution.py:54
  162.3 69.4 %reduce-scatter.2.cloned.1.call-start = ((), (), s32[]{:S(2)}) async-start(), calls=%async_computation.5 | async-start | bytes 2064384 | tf_op jit(solution)/shard_map/reduce_scatter | solution.py:162
  176.2 2.5 copy-start.5
  176.5 4.2 %copy-start.1 = (bf16[28,8,8,512]{3,1,2,0:T(8,128)(2,1)}, bf16[28,8,8,512]{3,1,2,0:T(8,128)(2,1)S(1)}, u32[]{:S(2)}) copy-start(bf16[28,8,8,512]{3,1,2,0:T(8,128)(2,1)S(1)} %copy.132) | copy-start | bytes 5505028
  178.7 1.9 copy-start.3
  237.9 15.5 %all-to-all-start.3 = ((bf16[32,2,1792]{2,1,0:T(2,128)(2,1)}), bf16[32,2,1792]{2,1,0:T(2,128)(2,1)S(1)}, u32[]{:S(2)}, u32[]{:S(2)}) async-start(bf16[32,2,1792]{2,1,0:T(2,128)(2,1)} %reshape.259), calls=%async_computation.4 | async-start | bytes 458752 | tf_op jit(solution)/shard_map/all_to_all | solution.py:165
Sparse Core Ops, SparseCore 0:
  162.4 12.1 all-gather.2
  187.5 44.1 reduce-scatter.1
